TPU v7x, 32 devices: a whole 2x2x4 slice. The times are simulated.
32 devices in a mesh: node: 32 (over z, y, x, core).
Axes of the slice: x: 2, y: 2, z: 4, core: 2. Of those that a mesh axis runs over, the one named last changes fastest.
Arguments:
- params: float32 [16384, 2048], P('node'), may hold values from -6 to 6
- public: float32 [16384, 2048], P('node'), may hold values from -4 to 4
- peer_public: float32 [16384, 2048], P('node'), may hold values from -8 to 8
- round_index: int32 [1], replicated, may hold values from 0 to 63
Outputs:
- params_new: float32 [16384, 2048], P('node')
- public_new: float32 [16384, 2048], P('node')
- peer_public_new: float32 [16384, 2048], P('node')
- consensus_gap: float32 [], replicated
All inputs are finite; a program needn't handle non-finite values.
Results may differ from a plain program's by a relative error of at most 0.0003.
Values may be sent and summed in bfloat16 or wider, within the bound.
A program may use at most 128 MiB of HBM per device.

v0:
```python
from functools import partial

import jax
import jax.numpy as jnp
from jax import lax
from jax.sharding import PartitionSpec as P

BLOCK = 128


def as_sent(value):
    return jax.tree.map(lambda a: a.astype(jnp.bfloat16) if a.dtype == jnp.float32 else a, value)


def partner(value, axis, stride):
    mask = 2**stride
    pairs = [(source, source ^ mask) for source in range(lax.axis_size(axis))]
    return lax.ppermute(value, axis, pairs)


def encode(params, public):
    row_count, col_count = params.shape
    difference = (params - public).reshape(row_count // BLOCK, BLOCK, col_count)
    block_peak = jnp.max(jnp.abs(difference), axis=1) + 1e-06
    block_scale = block_peak.astype(jnp.bfloat16)
    wide_scale = block_scale.astype(jnp.float32)[:, None, :]
    coded = jnp.floor(difference / wide_scale * 127.0 + 0.5).astype(jnp.bfloat16)
    own_delta = (coded.astype(jnp.float32) * wide_scale / 127.0).reshape(row_count, col_count)
    return (coded.reshape(row_count, col_count), block_scale, own_delta)


def decode(coded, block_scale):
    row_count, col_count = coded.shape
    wide_scale = block_scale.astype(jnp.float32)[:, None, :]
    shaped = coded.astype(jnp.float32).reshape(row_count // BLOCK, BLOCK, col_count)
    return (shaped * wide_scale / 127.0).reshape(row_count, col_count)


def swap_whole(bit, payload):
    return jax.tree.map(
        lambda part, own: part.astype(own.dtype), partner(as_sent(payload), "node", bit), payload
    )


def combine(params, public, peer_public, own_delta, partner_delta):
    public_new = public + own_delta
    peer_public_new = peer_public + partner_delta
    params_new = params + 0.4 * (peer_public_new - public_new)
    distance = params_new - public_new
    return (params_new, public_new, peer_public_new, jnp.sum(distance * distance))


def shards(params, public, peer_public, round_index):
    bit_count = lax.axis_size("node").bit_length() - 1
    chosen_bit = round_index[0] % bit_count
    row_count, col_count = params.shape
    coded, block_scale, own_delta = encode(params, public)
    branches = [partial(swap_whole, bit) for bit in range(bit_count)]
    got_coded, got_scale = lax.switch(chosen_bit, branches, (coded, block_scale))
    partner_delta = decode(got_coded, got_scale)
    params_new, public_new, peer_public_new, local_sum = combine(
        params, public, peer_public, own_delta, partner_delta
    )
    total = lax.psum(local_sum, "node")
    consensus_gap = total / jnp.float32(lax.axis_size("node") * row_count * col_count)
    return (params_new, public_new, peer_public_new, consensus_gap)


def solution(mesh):
    in_specs = (P("node", None), P("node", None), P("node", None), P())
    out_specs = (P("node", None), P("node", None), P("node", None), P())
    return jax.shard_map(shards, mesh=mesh, in_specs=in_specs, out_specs=out_specs, check_vma=False)
```

profile of v0, /device:TPU:0, one launch (start us, length us, event | category | flops | bytes accessed | tf_op | source)
XLA Modules:
  0.0 155.3 jit_solution(9956741445688569050)
XLA Ops:
  1.3 4.4 %bitcast_reduce_fusion = (f32[4,2048]{1,0:T(4,128)S(1)}, f32[512,2048]{1,0:T(8,128)S(1)}) fusion(f32[512,2048]{1,0:T(8,128)} %param.9, f32[512,2048]{1,0:T(8,128)} %param.10), kind=kLoop, calls=%fused_computation.10 | loop fusion | flops 3137536 | bytes 12615680 | tf_op jit(solution)/shard_map/reduce_max | solution.py:24
  5.7 0.7 fusion.7
  6.4 95.5 %conditional.4 = (bf16[4,2048]{1,0:T(4,128)(2,1)}, bf16[512,2048]{1,0:T(8,128)(2,1)}) conditional(s32[]{:T(128)} %clamp.3, (bf16[4,2048]{1,0:T(4,128)(2,1)S(1)}, bf16[512,2048]{1,0:T(8,128)(2,1)S(1)}) %tuple.50, (bf16[4,2048]{1,0:T(4,128)(2,1)S(1)}, bf16[512,2048]{1,0:T(8,128)(2,1)S(1)}) %tuple.50, ...), branch_computations={%region_1.2_spmd, %region_2.3_spmd, %region_3.4_spmd, %region_4.5_... | conditional | bytes 8454240
  6.4 4.1 %collective-permute-start.9 = (bf16[512,2048]{1,0:T(8,128)(2,1)S(1)}, bf16[512,2048]{1,0:T(8,128)(2,1)}, u32[]{:S(2)}, u32[]{:S(2)}) collective-permute-start(bf16[512,2048]{1,0:T(8,128)(2,1)S(1)} %get-tuple-element.37), channel_id=1, source_target_pairs={{0,16},{1,17},{2,18},{3,19},{4,20},{5,21},{6,22},{7,23},{8,24},{9,... | collective-permute-start | bytes 6291464 | tf_op jit(solution)/shard_map/cond/branch_4_fun/ppermute | solution.py:18
  10.6 0.1 collective-permute-start.8
  10.6 91.3 %collective-permute-done.8 = bf16[4,2048]{1,0:T(4,128)(2,1)} collective-permute-done((bf16[4,2048]{1,0:T(4,128)(2,1)S(1)}, bf16[4,2048]{1,0:T(4,128)(2,1)}, u32[]{:S(2)}, u32[]{:S(2)}) %collective-permute-start.8) | collective-permute-done | bytes 16416 | tf_op jit(solution)/shard_map/cond/branch_4_fun/ppermute | solution.py:18
  101.9 0.0 collective-permute-done.9
  101.9 0.7 convert_element_type.45
  102.7 10.9 %multiply_reduce_fusion = (f32[]{:T(128)}, f32[512,2048]{1,0:T(8,128)}, f32[512,2048]{1,0:T(8,128)}, f32[512,2048]{1,0:T(8,128)}) fusion(f32[512,2048]{1,0:T(8,128)} %param.9, f32[512,2048]{1,0:T(8,128)} %param.10, f32[4,2048]{1,0:T(4,128)S(1)} %get-tuple-element.54, bf16[512,2048]{1,0:T(8,128)(2,1)S(1)} %fusion.7, f32[512,2048]{1,0:T(8,128)} %param.11, ...), kind=kLoop, calls=%fused_computation.11 | loop fusion | flops 14680063 | bytes 29425668 | tf_op jit(solution)/shard_map/reduce_sum | solution.py:50
  113.6 40.0 %psum.7 = f32[]{:T(128)} all-reduce(f32[]{:T(128)} %get-tuple-element.50), channel_id=1, replica_groups=mesh['node'=32] {'node'}, use_global_device_ids=true, to_apply=%region_7.8 | all-reduce | flops 1 | bytes 8 | tf_op jit(solution)/shard_map/psum | solution.py:64
  (1 shorter events, 0.0 us)
Async XLA Ops:
  6.4 95.5 %collective-permute-start.9 = (bf16[512,2048]{1,0:T(8,128)(2,1)S(1)}, bf16[512,2048]{1,0:T(8,128)(2,1)}, u32[]{:S(2)}, u32[]{:S(2)}) collective-permute-start(bf16[512,2048]{1,0:T(8,128)(2,1)S(1)} %get-tuple-element.37), channel_id=1, source_target_pairs={{0,16},{1,17},{2,18},{3,19},{4,20},{5,21},{6,22},{7,23},{8,24},{9,... | collective-permute-start | bytes 6291464 | tf_op jit(solution)/shard_map/cond/branch_4_fun/ppermute | solution.py:18
  10.6 91.4 %collective-permute-start.8 = (bf16[4,2048]{1,0:T(4,128)(2,1)S(1)}, bf16[4,2048]{1,0:T(4,128)(2,1)}, u32[]{:S(2)}, u32[]{:S(2)}) collective-permute-start(bf16[4,2048]{1,0:T(4,128)(2,1)S(1)} %get-tuple-element.36), channel_id=1, source_target_pairs={{0,16},{1,17},{2,18},{3,19},{4,20},{5,21},{6,22},{7,23},{8,24},{9,... | collective-permute-start | bytes 49160 | tf_op jit(solution)/shard_map/cond/branch_4_fun/ppermute | solution.py:18
where the time goes:
time: 156 us; the launch traced here: 155 us
  waiting for transfers between devices  91.3 us (59%)
  blocking collectives  40 us (26%)
  other arithmetic  16.7 us (11%)
  starting transfers between devices  4.21 us (3%)
  between operations  3.1 us (2%)
    ppermute x2, waiting for transfers between devices, partner(): return lax.ppermute(value, axis, pairs)  91.3 us
    psum x1, blocking collectives, shards(): total = lax.psum(local_sum, 'node')  40 us
    reduce_sum x1, other arithmetic, combine(): jnp.sum(distance * distance)  10.9 us
    reduce_max x1, other arithmetic, encode(): block_peak = jnp.max(jnp.abs(difference), axis=1) + 1e-06  4.4 us
    ppermute x2, starting transfers between devices, partner(): return lax.ppermute(value, axis, pairs)  4.21 us
  transfers between devices with their start and end apart: 2, of which 1 were waited for; matrix products, arithmetic and copies ran while one was open for 0% of the time, Pallas kernels for 0%

commit v1 on v0

v1 whole, which is shorter than its diff:
```python
from functools import partial

import jax
import jax.numpy as jnp
from jax import lax
from jax.experimental import pallas as pl
from jax.experimental.pallas import tpu as pltpu
from jax.sharding import PartitionSpec as P

BLOCK = 128
MIX = 0.4


def chunk_list(row_count, col_count):
    blocks = row_count // BLOCK
    small = col_count // 4
    pieces = []
    for b in range(blocks):
        if b == 0:
            pieces += [(b, 0, 2 * small), (b, 2 * small, col_count - 2 * small)]
        elif b == blocks - 1:
            pieces += [(b, 0, col_count - small), (b, col_count - small, small)]
        else:
            pieces += [(b, 0, col_count)]
    return pieces


def enc_kernel(*refs):
    params_ref, public_ref = refs[:2]
    coded_ref, scale_ref, public_new_ref = refs[-3:]
    public = public_ref[...]
    difference = params_ref[...] - public
    peak = jnp.max(jnp.abs(difference), axis=0, keepdims=True) + 1e-06
    scale = peak.astype(jnp.bfloat16)
    wide = scale.astype(jnp.float32)
    level = jnp.floor(difference / wide * 127.0 + 0.5)
    coded_ref[...] = level.astype(jnp.bfloat16)
    scale_ref[...] = scale
    public_new_ref[...] = public + level * wide * (1.0 / 127.0)


def cost(count, reads, writes):
    return pl.CostEstimate(flops=12 * count, bytes_accessed=count * (reads + writes), transcendentals=0)


def encode(params, public, public_new, piece):
    b, c0, cw = piece
    tile = min(256, cw)
    base = c0 // tile
    here = pl.BlockSpec((BLOCK, tile), lambda j: (b, base + j))
    any_spec = pl.BlockSpec(memory_space=pl.ANY)
    args, specs, aliases = [params, public], [here, here], {}
    if public_new is not None:
        args.append(public_new)
        specs.append(any_spec)
        aliases = {2: 2}
    return pl.pallas_call(
        enc_kernel,
        grid=(cw // tile,),
        in_specs=specs,
        out_specs=[
            pl.BlockSpec((BLOCK, tile), lambda j: (0, j)),
            pl.BlockSpec((1, tile), lambda j: (0, j)),
            here,
        ],
        out_shape=[
            jax.ShapeDtypeStruct((BLOCK, cw), jnp.bfloat16),
            jax.ShapeDtypeStruct((1, cw), jnp.bfloat16),
            jax.ShapeDtypeStruct(params.shape, jnp.float32),
        ],
        input_output_aliases=aliases,
        cost_estimate=cost(BLOCK * cw, 8, 6),
        compiler_params=pltpu.CompilerParams(vmem_limit_bytes=8 << 20),
    )(*args)


def comb_kernel(params_ref, public_new_ref, peer_ref, coded_ref, scale_ref, acc_ref, *refs):
    params_out, peer_out, acc_out = refs[-3:]

    @pl.when(pl.program_id(0) == 0)
    def _():
        acc_out[...] = acc_ref[...]

    factor = scale_ref[...].astype(jnp.float32) * (1.0 / 127.0)
    peer_new = peer_ref[...] + coded_ref[...].astype(jnp.float32) * factor
    public_new = public_new_ref[...]
    params_new = params_ref[...] + MIX * (peer_new - public_new)
    peer_out[...] = peer_new
    params_out[...] = params_new
    distance = params_new - public_new
    square = distance * distance
    row = jnp.sum(square, axis=0, keepdims=True)
    total = row[:, :128]
    for k in range(1, row.shape[1] // 128):
        total += row[:, k * 128 : (k + 1) * 128]
    acc_out[...] += total


def combine(params, public_new, peer, coded, scale, acc, outs, piece):
    b, c0, cw = piece
    tile = min(256, cw)
    base = c0 // tile
    here = pl.BlockSpec((BLOCK, tile), lambda j: (b, base + j))
    whole = pl.BlockSpec((1, 128), lambda j: (0, 0))
    any_spec = pl.BlockSpec(memory_space=pl.ANY)
    args = [params, public_new, peer, coded, scale, acc]
    specs = [
        here,
        here,
        here,
        pl.BlockSpec((BLOCK, tile), lambda j: (0, j)),
        pl.BlockSpec((1, tile), lambda j: (0, j)),
        whole,
    ]
    aliases = {}
    if outs is not None:
        args += list(outs)
        specs += [any_spec, any_spec]
        aliases = {6: 0, 7: 1}
    full = jax.ShapeDtypeStruct(params.shape, jnp.float32)
    return pl.pallas_call(
        comb_kernel,
        grid=(cw // tile,),
        in_specs=specs,
        out_specs=[here, here, whole],
        out_shape=[full, full, jax.ShapeDtypeStruct((1, 128), jnp.float32)],
        input_output_aliases=aliases,
        cost_estimate=cost(BLOCK * cw, 14, 8),
        compiler_params=pltpu.CompilerParams(vmem_limit_bytes=8 << 20),
    )(*args)


def total_kernel(n, inverse, part_ref, out_ref, rows, send_sem, recv_sem):
    me = lax.axis_index("node")
    barrier = pltpu.get_barrier_semaphore()

    def greet(k, carry):
        pl.semaphore_signal(
            barrier, inc=1, device_id=(lax.rem(me + k, n),), device_id_type=pl.DeviceIdType.MESH
        )
        return carry

    lax.fori_loop(1, n, greet, 0)
    pl.semaphore_wait(barrier, n - 1)

    def copy(k):
        return pltpu.make_async_remote_copy(
            src_ref=part_ref,
            dst_ref=rows.at[me],
            send_sem=send_sem.at[k],
            recv_sem=recv_sem.at[me],
            device_id=(lax.rem(me + k, n),),
            device_id_type=pl.DeviceIdType.MESH,
        )

    def send(k, carry):
        copy(k).start()
        return carry

    lax.fori_loop(1, n, send, 0)
    rows[me] = part_ref[...]

    def arrive(k, carry):
        source = lax.rem(me + k, n)
        pltpu.make_async_remote_copy(
            src_ref=part_ref,
            dst_ref=rows.at[source],
            send_sem=send_sem.at[k],
            recv_sem=recv_sem.at[source],
            device_id=(source,),
            device_id_type=pl.DeviceIdType.MESH,
        ).wait()
        return carry

    lax.fori_loop(1, n, arrive, 0)
    summed = jnp.sum(rows[...], axis=0)
    out_ref[...] = jnp.broadcast_to(jnp.sum(summed, axis=1, keepdims=True) * inverse, out_ref.shape)


def total(part, n, count):
    return pl.pallas_call(
        partial(total_kernel, n, 1.0 / count),
        in_specs=[pl.BlockSpec(memory_space=pltpu.VMEM)],
        out_specs=pl.BlockSpec(memory_space=pltpu.VMEM),
        out_shape=jax.ShapeDtypeStruct((1, 128), jnp.float32),
        scratch_shapes=[
            pltpu.VMEM((n, 1, 128), jnp.float32),
            pltpu.SemaphoreType.DMA((n,)),
            pltpu.SemaphoreType.DMA((n,)),
        ],
        compiler_params=pltpu.CompilerParams(
            collective_id=0, has_side_effects=True, vmem_limit_bytes=4 << 20
        ),
    )(part)


def gossip(bit, params, public, peer_public):
    return gossip_round(bit, params, public, peer_public)


def gossip_round(bit, params, public, peer_public):
    n = lax.axis_size("node")
    pairs = [(source, source ^ (1 << bit)) for source in range(n)]
    pieces = chunk_list(*params.shape)
    public_new = None
    received = []
    for piece in pieces:
        coded, scale, public_new = encode(params, public, public_new, piece)
        got_scale = lax.ppermute(scale, "node", pairs)
        got_coded = lax.ppermute(coded, "node", pairs)
        received.append((got_coded, got_scale))
    acc = jnp.zeros((1, 128), jnp.float32)
    outs = None
    for piece, (coded, scale) in zip(pieces, received):
        params_new, peer_new, acc = combine(
            params, public_new, peer_public, coded, scale, acc, outs, piece
        )
        outs = (params_new, peer_new)
    return (*outs, public_new, acc)


def shards(params, public, peer_public, round_index):
    n = lax.axis_size("node")
    bit_count = n.bit_length() - 1
    chosen_bit = round_index[0] % bit_count
    row_count, col_count = params.shape
    branches = [partial(gossip, bit) for bit in range(bit_count)]
    params_new, peer_new, public_new, acc = lax.switch(
        chosen_bit, branches, params, public, peer_public
    )
    gap = total(acc, n, n * row_count * col_count)
    return (params_new, public_new, peer_new, gap[0, 0])


def solution(mesh):
    in_specs = (P("node", None), P("node", None), P("node", None), P())
    out_specs = (P("node", None), P("node", None), P("node", None), P())
    return jax.shard_map(shards, mesh=mesh, in_specs=in_specs, out_specs=out_specs, check_vma=False)
```

time: 156 us -> 154 us (0.987)
  Pallas kernels: 0 us -> 47.4 us
  blocking collectives: 40 us -> 0 us
  other arithmetic: 16.7 us -> 0 us
  starting transfers between devices: 4.21 us -> 15.8 us
  waiting for transfers between devices: 91.3 us -> 87.3 us
    pallas_call x0 -> x13, Pallas kernels: none -> 47.4 us  [the longest x6 23.7 us: combine(): pl.pallas_call(comb_kernel, grid=(cw // tile,), in_specs=specs, out_specs...]
    psum x1 -> x0, blocking collectives: 40 us -> none  [shards(): total = lax.psum(local_sum, 'node')]
    ppermute x2 -> x12, starting transfers between devices: 4.21 us -> 15.8 us  [the longest x6 9.94 us: gossip_round(): got_coded = lax.ppermute(coded, 'node', pairs)]
    reduce_sum x1 -> x0, other arithmetic: 10.9 us -> none  [combine(): jnp.sum(distance * distance)]
    reduce_max x1 -> x0, other arithmetic: 4.4 us -> none  [encode(): block_peak = jnp.max(jnp.abs(difference), axis=1) + 1e-06]
    ppermute x2 -> x12, waiting for transfers between devices: 91.3 us -> 87.3 us  [the longest x6 76.2 us: gossip_round(): got_scale = lax.ppermute(scale, 'node', pairs)]
  transfers between devices with their start and end apart: 2 -> 12, of which waited for: 1 -> 5; matrix products, arithmetic and copies ran while one was open for 0% -> 0% of each run, Pallas kernels for 0% -> 19%
where the time goes in v1:
time: 154 us; the launch traced here: 153 us
  waiting for transfers between devices  87.3 us (57%)
  Pallas kernels  47.4 us (31%)
  starting transfers between devices  15.8 us (10%)
  between operations  2.46 us (2%)
    ppermute x6, waiting for transfers between devices, gossip_round(): got_scale = lax.ppermute(scale, 'node', pairs)  76.2 us
    pallas_call x6, Pallas kernels, combine(): pl.pallas_call(comb_kernel, grid=(cw // tile,), in_specs=specs, out_specs...  23.7 us
    pallas_call x6, Pallas kernels, encode(): pl.pallas_call(enc_kernel, grid=(cw // tile,), in_specs=specs, out_specs=...  15.6 us
    ppermute x6, waiting for transfers between devices, gossip_round(): got_coded = lax.ppermute(coded, 'node', pairs)  11.1 us
    ppermute x6, starting transfers between devices, gossip_round(): got_coded = lax.ppermute(coded, 'node', pairs)  9.94 us
    pallas_call x1, Pallas kernels, total(): pl.pallas_call(partial(total_kernel, n, 1.0 / count), in_specs=[pl.BlockS...  8.13 us
    ppermute x6, starting transfers between devices, gossip_round(): got_scale = lax.ppermute(scale, 'node', pairs)  5.82 us
  transfers between devices with their start and end apart: 12, of which 5 were waited for; matrix products, arithmetic and copies ran while one was open for 0% of the time, Pallas kernels for 19%

profile of v1, /device:TPU:0, one launch (start us, length us, event | category | flops | bytes accessed | tf_op | source)
XLA Modules:
  0.0 153.2 jit_solution(3625013309443586939)
XLA Ops:
  1.3 142.6 %conditional.1 = (f32[512,2048]{1,0:T(8,128)}, f32[512,2048]{1,0:T(8,128)}, f32[512,2048]{1,0:T(8,128)}, f32[1,128]{1,0:T(1,128)S(1)}) conditional(s32[]{:T(128)} %clamp.3, (f32[512,2048]{1,0:T(8,128)}, f32[512,2048]{1,0:T(8,128)}, f32[512,2048]{1,0:T(8,128)}) %tuple.28, (f32[512,2048]{1,0:T(8,128)}, ...), branch_computations={%region_0.1_spmd, %region_1.2_spmd, %region_2.3_spmd, %region_3.4_... | conditional | flops 25165824 | bytes 96535648 | solution.py:228
  1.5 4.4 %branch_4_fun.12 = (bf16[128,1024]{1,0:T(8,128)(2,1)S(1)}, bf16[1,1024]{1,0:T(2,128)(2,1)S(1)}, f32[512,2048]{1,0:T(8,128)}) custom-call(f32[512,2048]{1,0:T(8,128)} %get-tuple-element.186.refs_0_.params_ref, f32[512,2048]{1,0:T(8,128)} %get-tuple-element.187.refs_1_), custom_call_target="tpu_custom_call" | custom-call | flops 1572864 | bytes 1835008 | tf_op jit(solution)/shard_map/cond/branch_4_fun/pallas_call | solution.py:57
  6.0 1.7 %branch_4_fun.13 = (bf16[128,1024]{1,0:T(8,128)(2,1)S(1)}, bf16[1,1024]{1,0:T(2,128)(2,1)S(1)}, f32[512,2048]{1,0:T(8,128)}) custom-call(f32[512,2048]{1,0:T(8,128)S(1)} %copy-done.4, f32[512,2048]{1,0:T(8,128)S(1)} %copy-done.9, f32[512,2048]{1,0:T(8,128)} %get-tuple-element.188.refs_2_), custom_call_target="tpu_custom_call", output_to_operand_aliasing={{2}: (2, {})} | custom-call | flops 1572864 | bytes 1835008 | tf_op jit(solution)/shard_map/cond/branch_4_fun/pallas_call | solution.py:57
  7.6 3.1 %branch_4_fun.14 = (bf16[128,2048]{1,0:T(8,128)(2,1)S(1)}, bf16[1,2048]{1,0:T(2,128)(2,1)S(1)}, f32[512,2048]{1,0:T(8,128)}) custom-call(f32[512,2048]{1,0:T(8,128)S(1)} %copy-done.4, f32[512,2048]{1,0:T(8,128)S(1)} %copy-done.9, f32[512,2048]{1,0:T(8,128)} %get-tuple-element.189.refs_2_), custom_call_target="tpu_custom_call", output_to_operand_aliasing={{2}: (2, {})} | custom-call | flops 3145728 | bytes 3670016 | tf_op jit(solution)/shard_map/cond/branch_4_fun/pallas_call | solution.py:57
  10.8 4.1 %collective-permute-start.54 = (bf16[128,2048]{1,0:T(8,128)(2,1)S(1)}, bf16[128,2048]{1,0:T(8,128)(2,1)S(1)}, u32[]{:S(2)}, u32[]{:S(2)}) collective-permute-start(bf16[128,2048]{1,0:T(8,128)(2,1)S(1)} %get-tuple-element.201), channel_id=1, source_target_pairs={{0,16},{1,17},{2,18},{3,19},{4,20},{5,21},{6,22},{7,23},{8,24},{9,... | collective-permute-start | bytes 1572872 | tf_op jit(solution)/shard_map/cond/branch_4_fun/ppermute | solution.py:210
  14.8 3.1 %branch_4_fun.15 = (bf16[128,2048]{1,0:T(8,128)(2,1)S(1)}, bf16[1,2048]{1,0:T(2,128)(2,1)S(1)}, f32[512,2048]{1,0:T(8,128)}) custom-call(f32[512,2048]{1,0:T(8,128)S(1)} %copy-done.4, f32[512,2048]{1,0:T(8,128)S(1)} %copy-done.9, f32[512,2048]{1,0:T(8,128)} %get-tuple-element.190.refs_2_), custom_call_target="tpu_custom_call", output_to_operand_aliasing={{2}: (2, {})} | custom-call | flops 3145728 | bytes 3670016 | tf_op jit(solution)/shard_map/cond/branch_4_fun/pallas_call | solution.py:57
  18.0 2.4 %branch_4_fun.16 = (bf16[128,1536]{1,0:T(8,128)(2,1)S(1)}, bf16[1,1536]{1,0:T(2,128)(2,1)S(1)}, f32[512,2048]{1,0:T(8,128)}) custom-call(f32[512,2048]{1,0:T(8,128)S(1)} %copy-done.4, f32[512,2048]{1,0:T(8,128)S(1)} %copy-done.9, f32[512,2048]{1,0:T(8,128)} %get-tuple-element.191.refs_2_), custom_call_target="tpu_custom_call", output_to_operand_aliasing={{2}: (2, {})} | custom-call | flops 2359296 | bytes 2752512 | tf_op jit(solution)/shard_map/cond/branch_4_fun/pallas_call | solution.py:57
  20.3 2.9 %collective-permute-start.50 = (bf16[128,1536]{1,0:T(8,128)(2,1)S(1)}, bf16[128,1536]{1,0:T(8,128)(2,1)S(1)}, u32[]{:S(2)}, u32[]{:S(2)}) collective-permute-start(bf16[128,1536]{1,0:T(8,128)(2,1)S(1)} %get-tuple-element.197), channel_id=1, source_target_pairs={{0,16},{1,17},{2,18},{3,19},{4,20},{5,21},{6,22},{7,23},{8,24},{9,... | collective-permute-start | bytes 1179656 | tf_op jit(solution)/shard_map/cond/branch_4_fun/ppermute | solution.py:210
  23.3 2.9 %collective-permute-start.59 = (bf16[1,1024]{1,0:T(2,128)(2,1)S(1)}, bf16[1,1024]{1,0:T(2,128)(2,1)S(1)}, u32[]{:S(2)}, u32[]{:S(2)}) collective-permute-start(bf16[1,1024]{1,0:T(2,128)(2,1)S(1)} %get-tuple-element.206), channel_id=1, source_target_pairs={{0,16},{1,17},{2,18},{3,19},{4,20},{5,21},{6,22},{7,23},{8,24},{9,... | collective-permute-start | bytes 6152 | tf_op jit(solution)/shard_map/cond/branch_4_fun/ppermute | solution.py:209
  26.2 62.5 %collective-permute-done.59.scale_ref = bf16[1,1024]{1,0:T(2,128)(2,1)S(1)} collective-permute-done((bf16[1,1024]{1,0:T(2,128)(2,1)S(1)}, bf16[1,1024]{1,0:T(2,128)(2,1)S(1)}, u32[]{:S(2)}, u32[]{:S(2)}) %collective-permute-start.59) | collective-permute-done | bytes 2080 | tf_op jit(solution)/shard_map/cond/branch_4_fun/ppermute | solution.py:209
  88.7 4.5 %collective-permute-done.57.scale_ref = bf16[1,1024]{1,0:T(2,128)(2,1)S(1)} collective-permute-done((bf16[1,1024]{1,0:T(2,128)(2,1)S(1)}, bf16[1,1024]{1,0:T(2,128)(2,1)S(1)}, u32[]{:S(2)}, u32[]{:S(2)}) %collective-permute-start.57) | collective-permute-done | bytes 2080 | tf_op jit(solution)/shard_map/cond/branch_4_fun/ppermute | solution.py:209
  93.2 4.5 %collective-permute-done.55.scale_ref = bf16[1,2048]{1,0:T(2,128)(2,1)S(1)} collective-permute-done((bf16[1,2048]{1,0:T(2,128)(2,1)S(1)}, bf16[1,2048]{1,0:T(2,128)(2,1)S(1)}, u32[]{:S(2)}, u32[]{:S(2)}) %collective-permute-start.55) | collective-permute-done | bytes 4128 | tf_op jit(solution)/shard_map/cond/branch_4_fun/ppermute | solution.py:209
  97.8 4.6 %collective-permute-done.53.scale_ref = bf16[1,2048]{1,0:T(2,128)(2,1)S(1)} collective-permute-done((bf16[1,2048]{1,0:T(2,128)(2,1)S(1)}, bf16[1,2048]{1,0:T(2,128)(2,1)S(1)}, u32[]{:S(2)}, u32[]{:S(2)}) %collective-permute-start.53) | collective-permute-done | bytes 4128 | tf_op jit(solution)/shard_map/cond/branch_4_fun/ppermute | solution.py:209
  102.4 0.9 branch_4_fun.17
  103.3 2.9 %collective-permute-start.48 = (bf16[128,512]{1,0:T(8,128)(2,1)S(1)}, bf16[128,512]{1,0:T(8,128)(2,1)S(1)}, u32[]{:S(2)}, u32[]{:S(2)}) collective-permute-start(bf16[128,512]{1,0:T(8,128)(2,1)S(1)} %get-tuple-element.195), channel_id=1, source_target_pairs={{0,16},{1,17},{2,18},{3,19},{4,20},{5,21},{6,22},{7,23},{8,24},{9,... | collective-permute-start | bytes 393224 | tf_op jit(solution)/shard_map/cond/branch_4_fun/ppermute | solution.py:210
  106.2 11.0 %collective-permute-done.58.coded_ref = bf16[128,1024]{1,0:T(8,128)(2,1)S(1)} collective-permute-done((bf16[128,1024]{1,0:T(8,128)(2,1)S(1)}, bf16[128,1024]{1,0:T(8,128)(2,1)S(1)}, u32[]{:S(2)}, u32[]{:S(2)}) %collective-permute-start.58) | collective-permute-done | bytes 262176 | tf_op jit(solution)/shard_map/cond/branch_4_fun/ppermute | solution.py:210
  117.3 3.3 %branch_4_fun.18 = (f32[512,2048]{1,0:T(8,128)}, f32[512,2048]{1,0:T(8,128)}, f32[1,128]{1,0:T(1,128)S(1)}) custom-call(f32[512,2048]{1,0:T(8,128)S(1)} %copy-done.4, f32[512,2048]{1,0:T(8,128)} %get-tuple-element.255.public_new_ref, f32[512,2048]{1,0:T(8,128)S(1)} %copy-done.14, bf16[128,1024]{1,0:T(8,128)(2,1)S(1)} %collective-permute-done.58.coded_ref, ...), custom_call_target="tpu_custom_call" | custom-call | flops 1572864 | bytes 2883584 | tf_op jit(solution)/shard_map/cond/branch_4_fun/pallas_call | solution.py:121
  120.6 3.3 %branch_4_fun.19 = (f32[512,2048]{1,0:T(8,128)}, f32[512,2048]{1,0:T(8,128)}, f32[1,128]{1,0:T(1,128)S(1)}) custom-call(f32[512,2048]{1,0:T(8,128)S(1)} %copy-done.4, f32[512,2048]{1,0:T(8,128)} %get-tuple-element.255.public_new_ref, f32[512,2048]{1,0:T(8,128)S(1)} %copy-done.14, ...), custom_call_target="tpu_custom_call", output_to_operand_aliasing={{0}: (6, {}), {1}: (7, {})} | custom-call | flops 1572864 | bytes 2883584 | tf_op jit(solution)/shard_map/cond/branch_4_fun/pallas_call | solution.py:121
  123.9 2.9 %collective-permute-start.49 = (bf16[1,512]{1,0:T(2,128)(2,1)S(1)}, bf16[1,512]{1,0:T(2,128)(2,1)S(1)}, u32[]{:S(2)}, u32[]{:S(2)}) collective-permute-start(bf16[1,512]{1,0:T(2,128)(2,1)S(1)} %get-tuple-element.196), channel_id=1, source_target_pairs={{0,16},{1,17},{2,18},{3,19},{4,20},{5,21},{6,22},{7,23},{8,24},{9,... | collective-permute-start | bytes 3080 | tf_op jit(solution)/shard_map/cond/branch_4_fun/ppermute | solution.py:209
  126.8 5.5 %branch_4_fun.20 = (f32[512,2048]{1,0:T(8,128)}, f32[512,2048]{1,0:T(8,128)}, f32[1,128]{1,0:T(1,128)S(1)}) custom-call(f32[512,2048]{1,0:T(8,128)S(1)} %copy-done.4, f32[512,2048]{1,0:T(8,128)} %get-tuple-element.255.public_new_ref, f32[512,2048]{1,0:T(8,128)S(1)} %copy-done.14, ...), custom_call_target="tpu_custom_call", output_to_operand_aliasing={{0}: (6, {}), {1}: (7, {})} | custom-call | flops 3145728 | bytes 5767168 | tf_op jit(solution)/shard_map/cond/branch_4_fun/pallas_call | solution.py:121
  132.3 5.5 %branch_4_fun.21 = (f32[512,2048]{1,0:T(8,128)}, f32[512,2048]{1,0:T(8,128)}, f32[1,128]{1,0:T(1,128)S(1)}) custom-call(f32[512,2048]{1,0:T(8,128)S(1)} %copy-done.4, f32[512,2048]{1,0:T(8,128)} %get-tuple-element.255.public_new_ref, f32[512,2048]{1,0:T(8,128)S(1)} %copy-done.14, ...), custom_call_target="tpu_custom_call", output_to_operand_aliasing={{0}: (6, {}), {1}: (7, {})} | custom-call | flops 3145728 | bytes 5767168 | tf_op jit(solution)/shard_map/cond/branch_4_fun/pallas_call | solution.py:121
  137.7 4.4 %branch_4_fun.22 = (f32[512,2048]{1,0:T(8,128)}, f32[512,2048]{1,0:T(8,128)}, f32[1,128]{1,0:T(1,128)S(1)}) custom-call(f32[512,2048]{1,0:T(8,128)S(1)} %copy-done.4, f32[512,2048]{1,0:T(8,128)} %get-tuple-element.255.public_new_ref, f32[512,2048]{1,0:T(8,128)S(1)} %copy-done.14, ...), custom_call_target="tpu_custom_call", output_to_operand_aliasing={{0}: (6, {}), {1}: (7, {})} | custom-call | flops 2359296 | bytes 4325376 | tf_op jit(solution)/shard_map/cond/branch_4_fun/pallas_call | solution.py:121
  142.2 1.8 %branch_4_fun.23 = (f32[512,2048]{1,0:T(8,128)}, f32[512,2048]{1,0:T(8,128)}, f32[1,128]{1,0:T(1,128)S(1)}) custom-call(f32[512,2048]{1,0:T(8,128)S(1)} %copy-done.4, f32[512,2048]{1,0:T(8,128)} %get-tuple-element.255.public_new_ref, f32[512,2048]{1,0:T(8,128)S(1)} %copy-done.14, ...), custom_call_target="tpu_custom_call", output_to_operand_aliasing={{0}: (6, {}), {1}: (7, {})} | custom-call | flops 786432 | bytes 1441792 | tf_op jit(solution)/shard_map/cond/branch_4_fun/pallas_call | solution.py:121
  143.9 8.1 %shard_map.75 = f32[1,128]{1,0:T(1,128)S(1)} custom-call(f32[1,128]{1,0:T(1,128)S(1)} %get-tuple-element.236.part_ref), custom_call_target="tpu_custom_call" | custom-call | tf_op jit(solution)/shard_map/pallas_call | solution.py:181
  (21 shorter events, 0.1 us)
Async XLA Ops:
  1.5 4.5 %copy-start.4 = (f32[512,2048]{1,0:T(8,128)S(1)}, f32[512,2048]{1,0:T(8,128)}, u32[]{:S(2)}) copy-start(f32[512,2048]{1,0:T(8,128)} %get-tuple-element.186.refs_0_.params_ref) | copy-start | bytes 12582916 | tf_op jit(solution)/shard_map/cond
  1.5 4.5 %copy-start.9 = (f32[512,2048]{1,0:T(8,128)S(1)}, f32[512,2048]{1,0:T(8,128)}, u32[]{:S(2)}) copy-start(f32[512,2048]{1,0:T(8,128)} %get-tuple-element.187.refs_1_) | copy-start | bytes 12582916 | tf_op jit(solution)/shard_map/cond
  10.8 113.1 %collective-permute-start.54 = (bf16[128,2048]{1,0:T(8,128)(2,1)S(1)}, bf16[128,2048]{1,0:T(8,128)(2,1)S(1)}, u32[]{:S(2)}, u32[]{:S(2)}) collective-permute-start(bf16[128,2048]{1,0:T(8,128)(2,1)S(1)} %get-tuple-element.201), channel_id=1, source_target_pairs={{0,16},{1,17},{2,18},{3,19},{4,20},{5,21},{6,22},{7,23},{8,24},{9,... | collective-permute-start | bytes 1572872 | tf_op jit(solution)/shard_map/cond/branch_4_fun/ppermute | solution.py:210
  18.0 114.3 %collective-permute-start.52 = (bf16[128,2048]{1,0:T(8,128)(2,1)S(1)}, bf16[128,2048]{1,0:T(8,128)(2,1)S(1)}, u32[]{:S(2)}, u32[]{:S(2)}) collective-permute-start(bf16[128,2048]{1,0:T(8,128)(2,1)S(1)} %get-tuple-element.199), channel_id=1, source_target_pairs={{0,16},{1,17},{2,18},{3,19},{4,20},{5,21},{6,22},{7,23},{8,24},{9,... | collective-permute-start | bytes 1572872 | tf_op jit(solution)/shard_map/cond/branch_4_fun/ppermute | solution.py:210
  20.3 117.4 %collective-permute-start.50 = (bf16[128,1536]{1,0:T(8,128)(2,1)S(1)}, bf16[128,1536]{1,0:T(8,128)(2,1)S(1)}, u32[]{:S(2)}, u32[]{:S(2)}) collective-permute-start(bf16[128,1536]{1,0:T(8,128)(2,1)S(1)} %get-tuple-element.197), channel_id=1, source_target_pairs={{0,16},{1,17},{2,18},{3,19},{4,20},{5,21},{6,22},{7,23},{8,24},{9,... | collective-permute-start | bytes 1179656 | tf_op jit(solution)/shard_map/cond/branch_4_fun/ppermute | solution.py:210
  23.3 80.0 %collective-permute-start.56 = (bf16[128,1024]{1,0:T(8,128)(2,1)S(1)}, bf16[128,1024]{1,0:T(8,128)(2,1)S(1)}, u32[]{:S(2)}, u32[]{:S(2)}) collective-permute-start(bf16[128,1024]{1,0:T(8,128)(2,1)S(1)} %get-tuple-element.203), channel_id=1, source_target_pairs={{0,16},{1,17},{2,18},{3,19},{4,20},{5,21},{6,22},{7,23},{8,24},{9,... | collective-permute-start | bytes 786440 | tf_op jit(solution)/shard_map/cond/branch_4_fun/ppermute | solution.py:210
  23.3 65.4 %collective-permute-start.59 = (bf16[1,1024]{1,0:T(2,128)(2,1)S(1)}, bf16[1,1024]{1,0:T(2,128)(2,1)S(1)}, u32[]{:S(2)}, u32[]{:S(2)}) collective-permute-start(bf16[1,1024]{1,0:T(2,128)(2,1)S(1)} %get-tuple-element.206), channel_id=1, source_target_pairs={{0,16},{1,17},{2,18},{3,19},{4,20},{5,21},{6,22},{7,23},{8,24},{9,... | collective-permute-start | bytes 6152 | tf_op jit(solution)/shard_map/cond/branch_4_fun/ppermute | solution.py:209
  88.7 4.5 %collective-permute-start.57 = (bf16[1,1024]{1,0:T(2,128)(2,1)S(1)}, bf16[1,1024]{1,0:T(2,128)(2,1)S(1)}, u32[]{:S(2)}, u32[]{:S(2)}) collective-permute-start(bf16[1,1024]{1,0:T(2,128)(2,1)S(1)} %get-tuple-element.204), channel_id=1, source_target_pairs={{0,16},{1,17},{2,18},{3,19},{4,20},{5,21},{6,22},{7,23},{8,24},{9,... | collective-permute-start | bytes 6152 | tf_op jit(solution)/shard_map/cond/branch_4_fun/ppermute | solution.py:209
  93.2 4.5 %collective-permute-start.55 = (bf16[1,2048]{1,0:T(2,128)(2,1)S(1)}, bf16[1,2048]{1,0:T(2,128)(2,1)S(1)}, u32[]{:S(2)}, u32[]{:S(2)}) collective-permute-start(bf16[1,2048]{1,0:T(2,128)(2,1)S(1)} %get-tuple-element.202), channel_id=1, source_target_pairs={{0,16},{1,17},{2,18},{3,19},{4,20},{5,21},{6,22},{7,23},{8,24},{9,... | collective-permute-start | bytes 12296 | tf_op jit(solution)/shard_map/cond/branch_4_fun/ppermute | solution.py:209
  97.8 4.6 %collective-permute-start.53 = (bf16[1,2048]{1,0:T(2,128)(2,1)S(1)}, bf16[1,2048]{1,0:T(2,128)(2,1)S(1)}, u32[]{:S(2)}, u32[]{:S(2)}) collective-permute-start(bf16[1,2048]{1,0:T(2,128)(2,1)S(1)} %get-tuple-element.200), channel_id=1, source_target_pairs={{0,16},{1,17},{2,18},{3,19},{4,20},{5,21},{6,22},{7,23},{8,24},{9,... | collective-permute-start | bytes 12296 | tf_op jit(solution)/shard_map/cond/branch_4_fun/ppermute | solution.py:209
  102.4 14.9 %collective-permute-start.58 = (bf16[128,1024]{1,0:T(8,128)(2,1)S(1)}, bf16[128,1024]{1,0:T(8,128)(2,1)S(1)}, u32[]{:S(2)}, u32[]{:S(2)}) collective-permute-start(bf16[128,1024]{1,0:T(8,128)(2,1)S(1)} %get-tuple-element.205), channel_id=1, source_target_pairs={{0,16},{1,17},{2,18},{3,19},{4,20},{5,21},{6,22},{7,23},{8,24},{9,... | collective-permute-start | bytes 786440 | tf_op jit(solution)/shard_map/cond/branch_4_fun/ppermute | solution.py:210
  102.4 14.9 %copy-start.14 = (f32[512,2048]{1,0:T(8,128)S(1)}, f32[512,2048]{1,0:T(8,128)}, u32[]{:S(2)}) copy-start(f32[512,2048]{1,0:T(8,128)} %get-tuple-element.194.peer_ref) | copy-start | bytes 12582916 | tf_op jit(solution)/shard_map/cond
  103.3 38.9 %collective-permute-start.48 = (bf16[128,512]{1,0:T(8,128)(2,1)S(1)}, bf16[128,512]{1,0:T(8,128)(2,1)S(1)}, u32[]{:S(2)}, u32[]{:S(2)}) collective-permute-start(bf16[128,512]{1,0:T(8,128)(2,1)S(1)} %get-tuple-element.195), channel_id=1, source_target_pairs={{0,16},{1,17},{2,18},{3,19},{4,20},{5,21},{6,22},{7,23},{8,24},{9,... | collective-permute-start | bytes 393224 | tf_op jit(solution)/shard_map/cond/branch_4_fun/ppermute | solution.py:210
  117.3 20.5 %collective-permute-start.51 = (bf16[1,1536]{1,0:T(2,128)(2,1)S(1)}, bf16[1,1536]{1,0:T(2,128)(2,1)S(1)}, u32[]{:S(2)}, u32[]{:S(2)}) collective-permute-start(bf16[1,1536]{1,0:T(2,128)(2,1)S(1)} %get-tuple-element.198), channel_id=1, source_target_pairs={{0,16},{1,17},{2,18},{3,19},{4,20},{5,21},{6,22},{7,23},{8,24},{9,... | collective-permute-start | bytes 9224 | tf_op jit(solution)/shard_map/cond/branch_4_fun/ppermute | solution.py:209
  123.9 18.3 %collective-permute-start.49 = (bf16[1,512]{1,0:T(2,128)(2,1)S(1)}, bf16[1,512]{1,0:T(2,128)(2,1)S(1)}, u32[]{:S(2)}, u32[]{:S(2)}) collective-permute-start(bf16[1,512]{1,0:T(2,128)(2,1)S(1)} %get-tuple-element.196), channel_id=1, source_target_pairs={{0,16},{1,17},{2,18},{3,19},{4,20},{5,21},{6,22},{7,23},{8,24},{9,... | collective-permute-start | bytes 3080 | tf_op jit(solution)/shard_map/cond/branch_4_fun/ppermute | solution.py:209
